TPU v7x, 32 devices: a whole 2x2x4 slice. The times are simulated.
32 devices in a mesh: role: 2 (over x), grp: 8 (over z, y), tp: 2 (over core).
Axes of the slice: x: 2, y: 2, z: 4, core: 2. Of those that a mesh axis runs over, the one named last changes fastest.
Arguments:
- q_new: bfloat16 [256, 4096], P('grp', ('role', 'tp')), may hold values from -9 to 9
- k_new: bfloat16 [256, 512], P('grp', ('role', 'tp')), may hold values from -6 to 6
- v_new: bfloat16 [256, 512], P('grp', ('role', 'tp')), may hold values from -6 to 6
- k_cache: bfloat16 [256, 128, 512], P('grp', None, ('role', 'tp')), may hold values from -9 to 9
- v_cache: bfloat16 [256, 128, 512], P('grp', None, ('role', 'tp')), may hold values from -6 to 6
- cache_len: int32 [256], P('grp'), may hold values from 1 to 127
- cycle_start: int32 [256], P('grp'), may hold values from 0 to 127
- residual: bfloat16 [256, 2880], P('grp', ('role', 'tp')), may hold values from -6 to 6
- out_proj: bfloat16 [4096, 2880], P(('role', 'tp')), may hold values from -0.09375 to 0.09375
- norm_gain: float32 [2880], replicated, may hold values from 0.25 to 1.75
- router: bfloat16 [2880, 8], P(('role', 'tp')), may hold values from -0.21875 to 0.21875
- route_ids: int32 [256, 4], P('grp'), may hold values from 0 to 7, all different within a row; in each aligned block of 32 rows (0 to 31, 32 to 63, ...) at most 18 rows name the same one
- w_gate: bfloat16 [8, 2880, 1440], P('grp', None, ('role', 'tp')), may hold values from -0.109375 to 0.109375
- w_up: bfloat16 [8, 2880, 1440], P('grp', None, ('role', 'tp')), may hold values from -0.109375 to 0.109375
- w_down: bfloat16 [8, 1440, 2880], P('grp', ('role', 'tp')), may hold values from -0.15625 to 0.15625
Outputs:
- attended: bfloat16 [256, 2880], P('grp', ('role', 'tp'))
- expert_mix: bfloat16 [256, 2880], P('grp', ('role', 'tp'))
Inputs may be any that keep to these rules, and one draw needn't show every extreme that they name: `route_ids`: the 4 experts of a token differ. Among the tokens of one grp index (aligned blocks of 32 tokens) no expert is named more than 18 times, a bound that some block reaches.
All inputs are finite; a program needn't handle non-finite values.
Results may differ from a plain program's by a relative error of at most 0.017.
Values may be sent and summed in bfloat16 or wider, within the bound.
No kernel may reach another device: no remote copies, remote signals or barrier semaphores. Data moves between devices by JAX's collectives and lax.ppermute only.
A program may use at most 64 MiB of HBM per device.

v0:
```python
import jax
import jax.numpy as jnp
from jax import lax
from jax.sharding import PartitionSpec as P

HEADS = 64
KV_HEADS = 8
HD = 64
epsilon = 1e-05


def attend(q_new, k_new, v_new, k_cache, v_cache, cache_len, cycle_start):
    tokens = q_new.shape[0]
    window = k_cache.shape[1]
    kv_local = k_new.shape[1] // HD
    grouped = HEADS // KV_HEADS
    queries = q_new.reshape(tokens, kv_local, grouped, HD)
    cached_keys = k_cache.reshape(tokens, window, kv_local, HD)
    cached_values = v_cache.reshape(tokens, window, kv_local, HD)
    own_key = k_new.reshape(tokens, kv_local, HD)
    own_value = v_new.reshape(tokens, kv_local, HD)
    factor = HD ** (-0.5)
    scores = (
        jnp.einsum("tkgd,tskd->tkgs", queries, cached_keys, preferred_element_type=jnp.float32)
        * factor
    )
    own_score = (
        jnp.einsum("tkgd,tkd->tkg", queries, own_key, preferred_element_type=jnp.float32) * factor
    )
    positions = jnp.arange(window, dtype=jnp.int32)
    usable = (positions[None, :] - cycle_start[:, None]) % window < cache_len[:, None]
    usable = usable[:, None, None, :]
    masked = jnp.where(usable, scores, -1e30)
    highest = jnp.maximum(jnp.max(masked, axis=3), own_score)
    lifted = jnp.where(usable, jnp.exp(masked - highest[..., None]), 0.0)
    own_lift = jnp.exp(own_score - highest)
    denominator = jnp.sum(lifted, axis=3) + own_lift
    weights = (lifted / denominator[..., None]).astype(jnp.bfloat16)
    own_weight = (own_lift / denominator).astype(jnp.bfloat16)
    combined = jnp.einsum(
        "tkgs,tskd->tkgd", weights, cached_values, preferred_element_type=jnp.float32
    )
    combined = (
        combined
        + own_weight.astype(jnp.float32)[..., None] * own_value.astype(jnp.float32)[:, :, None, :]
    )
    return combined.reshape(tokens, -1).astype(jnp.bfloat16)


def slot_tables(route_ids, logits, capacity):
    experts_count = logits.shape[1]
    named = route_ids[:, :, None] == jnp.arange(experts_count, dtype=jnp.int32)
    chosen = jnp.sum(jnp.where(named, logits[:, None, :], 0.0), axis=2)
    lifted = jnp.exp(chosen)
    route_weight = lifted / jnp.sum(lifted, axis=1, keepdims=True)
    counts = jnp.sum(named.astype(jnp.int32), axis=1)
    earlier = jnp.cumsum(counts, axis=0) - counts
    ranks = jnp.sum(jnp.where(named, earlier[:, None, :], 0), axis=2)
    placed = named[:, :, :, None] & (
        ranks[:, :, None, None] == jnp.arange(capacity, dtype=jnp.int32)
    )
    select = jnp.sum(placed.astype(jnp.float32), axis=1).reshape(route_ids.shape[0], -1)
    mixing = jnp.sum(jnp.where(placed, route_weight[:, :, None, None], 0.0), axis=1).reshape(
        route_ids.shape[0], -1
    )
    return (select, mixing)


def serve(received, w_gate, w_up, w_down):
    sources = received.shape[0]
    items = received.shape[1]
    inputs = received.reshape(sources * items, received.shape[2])
    gate_lin = jnp.dot(inputs, w_gate[0], preferred_element_type=jnp.float32)
    up_lin = jnp.dot(inputs, w_up[0], preferred_element_type=jnp.float32)
    activated = (gate_lin * jax.nn.sigmoid(1.702 * gate_lin) * (up_lin + 1.0)).astype(jnp.bfloat16)
    partial_out = jnp.dot(activated, w_down[0], preferred_element_type=jnp.float32).reshape(
        sources, items, -1
    )
    rounded = lax.optimization_barrier(partial_out.astype(jnp.bfloat16))
    return lax.all_to_all(rounded, "grp", split_axis=0, concat_axis=0, tiled=True)


def local(
    q_new,
    k_new,
    v_new,
    k_cache,
    v_cache,
    cache_len,
    cycle_start,
    residual,
    out_proj,
    norm_gain,
    router,
    route_ids,
    w_gate,
    w_up,
    w_down,
):
    share = lax.axis_index(("role", "tp"))
    quarter = residual.shape[1]
    heads_out = attend(q_new, k_new, v_new, k_cache, v_cache, cache_len, cycle_start)
    projected = jnp.dot(heads_out, out_proj, preferred_element_type=jnp.float32)
    stream = lax.all_gather(residual, ("role", "tp"), axis=1, tiled=True).astype(
        jnp.float32
    ) + lax.psum(projected.astype(jnp.bfloat16), ("role", "tp")).astype(jnp.float32)
    scale = lax.rsqrt(jnp.mean(stream * stream, axis=1, keepdims=True) + epsilon)
    outgoing = (stream * scale * norm_gain).astype(jnp.bfloat16)
    own_normed = lax.dynamic_slice_in_dim(outgoing, share * quarter, quarter, 1)
    attended = lax.dynamic_slice_in_dim(stream, share * quarter, quarter, 1)
    logits = lax.psum(
        jnp.dot(own_normed, router, preferred_element_type=jnp.float32), ("role", "tp")
    )
    tokens = route_ids.shape[0]
    experts_count = logits.shape[1]
    capacity = max(3, tokens * route_ids.shape[1] // experts_count + 2)
    select, mixing = slot_tables(route_ids, logits, capacity)
    outbound = jnp.einsum(
        "ts,tf->sf", select.astype(jnp.bfloat16), outgoing, preferred_element_type=jnp.float32
    )
    outbound = outbound.astype(jnp.bfloat16).reshape(experts_count, capacity, -1)
    returned = serve(
        lax.all_to_all(outbound, "grp", split_axis=0, concat_axis=0, tiled=True),
        w_gate,
        w_up,
        w_down,
    )
    stacked = returned.reshape(-1, returned.shape[2]).astype(jnp.float32)
    combined = jnp.dot(mixing, stacked, precision=lax.Precision.HIGHEST)
    combined = lax.psum_scatter(
        combined.astype(jnp.bfloat16), ("role", "tp"), scatter_dimension=1, tiled=True
    ).astype(jnp.float32)
    return (attended.astype(jnp.bfloat16), combined.astype(jnp.bfloat16))


def solution(mesh):
    placed = (
        P("grp", ("role", "tp")),
        P("grp", ("role", "tp")),
        P("grp", ("role", "tp")),
        P("grp", None, ("role", "tp")),
        P("grp", None, ("role", "tp")),
        P("grp"),
        P("grp"),
        P("grp", ("role", "tp")),
        P(("role", "tp"), None),
        P(),
        P(("role", "tp"), None),
        P("grp", None),
        P("grp", None, ("role", "tp")),
        P("grp", None, ("role", "tp")),
        P("grp", ("role", "tp"), None),
    )
    return jax.shard_map(
        local,
        mesh=mesh,
        in_specs=placed,
        out_specs=(P("grp", ("role", "tp")), P("grp", ("role", "tp"))),
        check_vma=False,
    )
```

profile of v0, /device:TPU:0, one launch (start us, length us, event | category | flops | bytes accessed | tf_op | source)
XLA Modules:
  0.0 172.5 jit_solution(14774596593833444122)
XLA Ops:
  7.2 0.9 reshape.146
  8.9 1.0 reshape.131
  10.7 1.6 copy.52
  12.4 1.4 fusion.37
  15.1 1.6 copy.57
  16.8 2.1 %fusion.13 = bf16[32,2,8,64]{3,2,1,0:T(8,128)(2,1)} fusion(bf16[32,128,2,64]{1,3,2,0:T(8,128)(2,1)S(1)} %bitcast.66, f32[32,2,8,128]{3,2,1,0:T(8,128)S(1)} %get-tuple-element.9, f32[32,2,64]{2,1,0:T(2,128)S(1)} %reshape.137, f32[32,2,8]{2,1,0:T(2,128)} %copy.58, f32[32,2,8]{2,1,0:T(2,128)S(1)} %copy.56, f32[32,2,8]{2,1,0:T(2,128)S(1)} %copy.54, ...), kind=kOutput, calls=%fused_computation.15 | convolution fusion | flops 8749056 | bytes 1402880 | tf_op jit(solution)/shard_map/tkgs,tskd->tkgd/dot_general | solution.py:40
  18.9 1.0 convert_element_type.74
  20.0 5.2 %convolution_convert_fusion.2 = bf16[32,2880]{1,0:T(8,128)(2,1)} fusion(bf16[32,1024]{1,0:T(8,128)(2,1)S(1)} %convert_element_type.74, bf16[1024,2880]{0,1:T(8,128)(2,1)} %param.23), kind=kOutput, calls=%fused_computation.4 | convolution fusion | flops 188835840 | bytes 6148096 | tf_op jit(solution)/shard_map/dot_general | solution.py:103
  25.6 6.9 %all-gather = bf16[4,720,32]{1,2,0:T(8,128)(2,1)S(1)} all-gather(bf16[1,720,32]{1,2,0:T(8,128)(2,1)S(1)} %bitcast.68), channel_id=1, replica_groups=mesh['role'=2,'grp'=8,'tp'=2] {'role','tp'}, dimensions={0}, use_global_device_ids=true | all-gather | bytes 230400 | tf_op jit(solution)/shard_map/all_gather | solution.py:104
  32.9 27.2 %all-reduce.2.cloned.1.call-done = bf16[32,2880]{1,0:T(8,128)(2,1)} async-done(((bf16[32,2880]{1,0:T(8,128)(2,1)}), bf16[32,2880]{1,0:T(8,128)(2,1)}) %all-reduce.2.cloned.1.call-update) | async-done | bytes 184336 | tf_op jit(solution)/shard_map/psum | solution.py:106
  60.0 1.1 multiply_reduce_fusion
  62.2 5.7 %psum.15 = f32[32,8]{0,1:T(8,128)S(1)} all-reduce(f32[32,8]{0,1:T(8,128)S(1)} %fusion.25), channel_id=1, replica_groups=mesh['role'=2,'grp'=8,'tp'=2] {'role','tp'}, use_global_device_ids=true, to_apply=%region_7.8 | all-reduce | flops 256 | bytes 2048 | tf_op jit(solution)/shard_map/psum | solution.py:111
  68.4 1.3 convolution_convert_fusion.1
  69.7 1.4 reshape.135
  71.1 33.4 %all_to_all.10 = bf16[8,18,2880]{2,1,0:T(8,128)(2,1)} all-to-all(bf16[8,18,2880]{2,1,0:T(8,128)(2,1)S(1)} %reshape.135), channel_id=1, replica_groups=mesh['role'=2,'grp'=8,'tp'=2] {'grp'}, dimensions={0} | all-to-all | bytes 1658880 | tf_op jit(solution)/shard_map/all_to_all | solution.py:123
  104.6 1.7 reshape.136
  106.3 2.6 %fusion.4 = f32[144,360]{1,0:T(8,128)S(1)} fusion(bf16[144,2880]{1,0:T(8,128)(2,1)S(1)} %reshape.136, bf16[1,2880,360]{1,2,0:T(8,128)(2,1)} %param.27), kind=kOutput, calls=%fused_computation.8 | convolution fusion | flops 298598400 | bytes 3110400 | tf_op jit(solution)/shard_map/dot_general | solution.py:73
  108.9 0.8 fusion.14
  110.6 30.5 %all_to_all.11 = bf16[8,18,2880]{2,1,0:T(8,128)(2,1)S(1)} all-to-all(bf16[8,18,2880]{2,1,0:T(8,128)(2,1)S(1)} %convolution_convert_fusion), channel_id=1, replica_groups=mesh['role'=2,'grp'=8,'tp'=2] {'grp'}, dimensions={0} | all-to-all | bytes 1658880 | tf_op jit(solution)/shard_map/all_to_all | solution.py:80
  141.1 0.8 fusion
  141.9 1.2 copy.66
  143.1 1.6 dynamic-slice_convert_fusion
  144.7 19.3 %reduce-scatter.4.cloned.1.call-done = bf16[720,32]{1,0:T(8,128)(2,1)} async-done(((bf16[2880,32]{1,0:T(8,128)(2,1)}), bf16[720,32]{1,0:T(8,128)(2,1)}) %reduce-scatter.4.cloned.1.call-update) | async-done | bytes 46096
  164.0 1.7 copy.67
  (57 shorter events, 6.0 us)
Async XLA Ops:
  7.2 102.6 %copy-start = (bf16[1,360,2880]{2,1,0:T(8,128)(2,1)S(1)}, bf16[1,360,2880]{2,1,0:T(8,128)(2,1)}, u32[]{:S(2)}) copy-start(bf16[1,360,2880]{2,1,0:T(8,128)(2,1)} %param.29) | copy-start | bytes 6220804
  7.2 5.1 %copy-start.8 = (s32[32]{0:T(128)S(1)}, s32[32]{0:T(128)}, u32[]{:S(2)}) copy-start(s32[32]{0:T(128)} %param.21) | copy-start | bytes 388
  7.2 5.1 %copy-start.7 = (s32[32]{0:T(128)S(1)}, s32[32]{0:T(128)}, u32[]{:S(2)}) copy-start(s32[32]{0:T(128)} %param.20) | copy-start | bytes 388
  7.2 52.8 %all-reduce.2.cloned.1.call-start = ((), (), s32[]{:S(2)}) async-start(), calls=%async_computation.3 | async-start | bytes 376832 | tf_op jit(solution)/shard_map/psum | solution.py:106
  10.0 0.6 copy-start.2
  19.9 5.3 %copy-start.4 = (s32[32,4]{0,1:T(4,128)S(1)}, s32[32,4]{0,1:T(4,128)}, u32[]{:S(2)}) copy-start(s32[32,4]{0,1:T(4,128)} %param.26) | copy-start | bytes 1540
  20.0 5.6 %copy-start.3 = (bf16[32,720]{1,0:T(8,128)(2,1)S(1)}, bf16[32,720]{1,0:T(8,128)(2,1)}, u32[]{:S(2)}) copy-start(bf16[32,720]{1,0:T(8,128)(2,1)} %param.22) | copy-start | bytes 138244
  25.2 36.7 %copy-start.6 = (f32[2880]{0:T(1024)S(1)}, f32[2880]{0:T(1024)}, u32[]{:S(2)}) copy-start(f32[2880]{0:T(1024)} %param.24) | copy-start | bytes 34564
  25.2 36.8 %copy-start.5 = (bf16[720,8]{0,1:T(8,128)(2,1)S(1)}, bf16[720,8]{0,1:T(8,128)(2,1)}, u32[]{:S(2)}) copy-start(bf16[720,8]{0,1:T(8,128)(2,1)} %param.25) | copy-start | bytes 34564
  25.2 138.8 %reduce-scatter.4.cloned.1.call-start = ((), (), s32[]{:S(2)}) async-start(), calls=%async_computation.4 | async-start | bytes 921600
  61.1 0.8 copy-start.1
  106.3 2.6 %copy-start.9 = (bf16[1,2880,360]{1,2,0:T(8,128)(2,1)S(1)}, bf16[1,2880,360]{1,2,0:T(8,128)(2,1)}, u32[]{:S(2)}) copy-start(bf16[1,2880,360]{1,2,0:T(8,128)(2,1)} %param.28) | copy-start | bytes 6220804
Sparse Core Ops, SparseCore 0:
  25.3 34.6 all-reduce.1
  143.2 20.7 reduce-scatter.3
where the time goes:
time: 173 us
  blocking collectives  76.6 us (44%)
  waiting for transfers between devices  46.5 us (27%)
  local copies, waits for them, and re-layouts  17.7 us (10%)
  matrix products  15.4 us (9%)
  between operations  14.3 us (8%)
  other arithmetic  1.84 us (1%)
    all_to_all x1, blocking collectives, local(): lax.all_to_all(outbound, 'grp', split_axis=0, concat_axis=0, tiled=True)  33.4 us
    all_to_all x1, blocking collectives, serve(): lax.all_to_all(rounded, 'grp', split_axis=0, concat_axis=0, tiled=True)  30.5 us
    psum x1, waiting for transfers between devices, local(): lax.psum(projected.astype(jnp.bfloat16), ('role', 'tp')).astype(jnp.float32)  27.2 us
    unnamed x3, waiting for transfers between devices  19.3 us
    unnamed x24, local copies, waits for them, and re-layouts  7.26 us
    all_gather x1, blocking collectives, local(): lax.all_gather(residual, ('role', 'tp'), axis=1, tiled=True)  6.87 us
    psum x1, blocking collectives, local(): lax.psum(jnp.dot(own_normed, router, preferred_element_type=jnp.float32),...  5.74 us
    dot_general x1, matrix products, local(): projected = jnp.dot(heads_out, out_proj, preferred_element_type=jnp.float32)  5.22 us
  transfers between devices with their start and end apart: 2, of which 2 were waited for; matrix products, arithmetic and copies ran while one was open for 1% of the time, Pallas kernels for 0%

commit v1 on v0

--- a/solution.py
+++ b/solution.py
@@ -7,6 +7,7 @@
 KV_HEADS = 8
 HD = 64
 epsilon = 1e-05
+step_on_zone = lambda patch: jnp.sum(lax.all_gather(patch, ("role", "tp")), axis=0)
 
 
 def attend(q_new, k_new, v_new, k_cache, v_cache, cache_len, cycle_start):
@@ -103,7 +104,7 @@
     projected = jnp.dot(heads_out, out_proj, preferred_element_type=jnp.float32)
     stream = lax.all_gather(residual, ("role", "tp"), axis=1, tiled=True).astype(
         jnp.float32
-    ) + lax.psum(projected.astype(jnp.bfloat16), ("role", "tp")).astype(jnp.float32)
+    ) + step_on_zone(projected.astype(jnp.bfloat16)).astype(jnp.float32)
     scale = lax.rsqrt(jnp.mean(stream * stream, axis=1, keepdims=True) + epsilon)
     outgoing = (stream * scale * norm_gain).astype(jnp.bfloat16)
     own_normed = lax.dynamic_slice_in_dim(outgoing, share * quarter, quarter, 1)

time: 173 us -> 162 us (0.936)
  waiting for transfers between devices: 46.5 us -> 19.9 us
  blocking collectives: 76.6 us -> 85.9 us
  other arithmetic: 1.84 us -> 6.06 us
    psum x1 -> x0, waiting for transfers between devices: 27.2 us -> none  [local(): lax.psum(projected.astype(jnp.bfloat16), ('role', 'tp')).astype(jnp.float32)]
    all_gather x0 -> x1, blocking collectives: none -> 8.76 us  [lax.all_gather(patch, ('role', 'tp'))]
    unnamed x24 -> x28, local copies, waits for them, and re-layouts: 7.26 us -> 6.49 us
    unnamed x3 -> x2, waiting for transfers between devices: 19.3 us -> 19.9 us
  transfers between devices with their start and end apart: 2 -> 1, of which waited for: 2 -> 1; matrix products, arithmetic and copies ran while one was open for 1% -> 1% of each run, Pallas kernels for 0% -> 0%
where the time goes in v1:
time: 162 us; the launch traced here: 161 us
  blocking collectives  85.9 us (53%)
  waiting for transfers between devices  19.9 us (12%)
  local copies, waits for them, and re-layouts  18.8 us (12%)
  matrix products  16.2 us (10%)
  between operations  14.3 us (9%)
  other arithmetic  6.06 us (4%)
    all_to_all x1, blocking collectives, local(): lax.all_to_all(outbound, 'grp', split_axis=0, concat_axis=0, tiled=True)  32.5 us
    all_to_all x1, blocking collectives, serve(): lax.all_to_all(rounded, 'grp', split_axis=0, concat_axis=0, tiled=True)  30.4 us
    unnamed x2, waiting for transfers between devices  19.9 us
    all_gather x1, blocking collectives, lax.all_gather(patch, ('role', 'tp'))  8.76 us
    psum x1, blocking collectives, local(): lax.psum(jnp.dot(own_normed, router, preferred_element_type=jnp.float32),...  7.18 us
    all_gather x1, blocking collectives, local(): lax.all_gather(residual, ('role', 'tp'), axis=1, tiled=True)  7.06 us
    unnamed x28, local copies, waits for them, and re-layouts  6.49 us
    dot_general x1, matrix products, local(): projected = jnp.dot(heads_out, out_proj, preferred_element_type=jnp.float32)  4.51 us
  transfers between devices with their start and end apart: 1, of which 1 were waited for; matrix products, arithmetic and copies ran while one was open for 1% of the time, Pallas kernels for 0%

profile of v1, /device:TPU:0, one launch (start us, length us, event | category | flops | bytes accessed | tf_op | source)
XLA Modules:
  0.0 161.2 jit_solution(11152564190663925649)
XLA Ops:
  7.2 0.8 convert_reduce_fusion
  8.1 1.3 iota_compare_fusion.1
  11.6 1.4 reshape.137
  13.0 1.0 reshape.131
  14.7 7.1 %all-gather.1 = bf16[4,720,32]{1,2,0:T(8,128)(2,1)S(1)} all-gather(bf16[1,720,32]{1,2,0:T(8,128)(2,1)} %bitcast.70), channel_id=1, replica_groups=mesh['role'=2,'grp'=8,'tp'=2] {'role','tp'}, dimensions={0}, use_global_device_ids=true | all-gather | bytes 230400 | tf_op jit(solution)/shard_map/all_gather | solution.py:105
  22.2 1.6 %copy.56 = bf16[32,128,128]{1,2,0:T(8,128)(2,1)S(1)} copy(bf16[32,128,128]{2,1,0:T(8,128)(2,1)} %param.18) | data formatting | bytes 2097152 | tf_op args[3]
  24.6 2.6 %fusion.37 = (f32[32,2,8]{2,1,0:T(2,128)}, f32[32,2,8,128]{3,2,1,0:T(8,128)}) fusion(bf16[32,2,8,64]{3,2,1,0:T(8,128)(2,1)} %copy-done.2, bf16[32,128,2,64]{1,3,2,0:T(8,128)(2,1)S(1)} %bitcast.65, pred[32,128]{1,0:T(8,128)(4,1)S(1)} %fusion.28), kind=kOutput, calls=%fused_computation.59 | convolution fusion | flops 8584704 | bytes 1382400 | tf_op jit(solution)/shard_map/tkgd,tskd->tkgs/dot_general | solution.py:25
  28.1 1.2 fusion.19
  30.8 1.6 %copy.61 = bf16[32,128,128]{1,2,0:T(8,128)(2,1)S(1)} copy(bf16[32,128,128]{2,1,0:T(8,128)(2,1)} %param.19) | data formatting | bytes 2097152 | tf_op args[4]
  32.5 2.4 %fusion.13 = bf16[32,2,8,64]{3,2,1,0:T(8,128)(2,1)} fusion(bf16[32,128,2,64]{1,3,2,0:T(8,128)(2,1)S(1)} %bitcast.68, f32[32,2,8,128]{3,2,1,0:T(8,128)} %get-tuple-element.9, f32[32,2,64]{2,1,0:T(2,128)} %reshape.137, f32[32,2,8]{2,1,0:T(2,128)} %copy.62, f32[32,2,8]{2,1,0:T(2,128)} %copy.60, f32[32,2,8]{2,1,0:T(2,128)} %copy-done.3, ...), kind=kOutput, calls=%fused_computation.15 | convolution fusion | flops 8749056 | bytes 1402880 | tf_op jit(solution)/shard_map/tkgs,tskd->tkgd/dot_general | solution.py:41
  34.9 1.0 convert_element_type.76
  35.9 4.5 %convolution_convert_fusion.2 = bf16[32,2880]{1,0:T(8,128)(2,1)S(1)} fusion(bf16[32,1024]{1,0:T(8,128)(2,1)S(1)} %convert_element_type.76, bf16[1024,2880]{0,1:T(8,128)(2,1)} %param.23), kind=kOutput, calls=%fused_computation.4 | convolution fusion | flops 188835840 | bytes 6148096 | tf_op jit(solution)/shard_map/dot_general | solution.py:104
  40.5 8.8 %all-gather = bf16[128,2880]{1,0:T(8,128)(2,1)S(1)} all-gather(bf16[32,2880]{1,0:T(8,128)(2,1)S(1)} %convolution_convert_fusion.2), channel_id=2, replica_groups=mesh['role'=2,'grp'=8,'tp'=2] {'role','tp'}, dimensions={0}, use_global_device_ids=true | all-gather | bytes 921600 | tf_op jit(solution)/shard_map/all_gather | solution.py:10
  49.9 7.2 %psum.7 = f32[32,8]{0,1:T(8,128)S(1)} all-reduce(f32[32,8]{0,1:T(8,128)S(1)} %fusion.25), channel_id=1, replica_groups=mesh['role'=2,'grp'=8,'tp'=2] {'role','tp'}, use_global_device_ids=true, to_apply=%region_7.8 | all-reduce | flops 256 | bytes 2048 | tf_op jit(solution)/shard_map/psum | solution.py:112
  57.5 1.3 convolution_convert_fusion.1
  58.8 1.4 reshape.135
  60.3 32.5 %all_to_all.10 = bf16[8,18,2880]{2,1,0:T(8,128)(2,1)} all-to-all(bf16[8,18,2880]{2,1,0:T(8,128)(2,1)S(1)} %reshape.135), channel_id=1, replica_groups=mesh['role'=2,'grp'=8,'tp'=2] {'grp'}, dimensions={0} | all-to-all | bytes 1658880 | tf_op jit(solution)/shard_map/all_to_all | solution.py:124
  92.8 1.7 %reshape.136 = bf16[144,2880]{1,0:T(8,128)(2,1)S(1)} reshape(bf16[8,18,2880]{2,1,0:T(8,128)(2,1)} %all_to_all.10) | data formatting | bytes 1658880 | tf_op jit(solution)/shard_map/reshape | solution.py:73
  94.5 2.6 %fusion.4 = f32[144,360]{1,0:T(8,128)S(1)} fusion(bf16[144,2880]{1,0:T(8,128)(2,1)S(1)} %reshape.136, bf16[1,2880,360]{1,2,0:T(8,128)(2,1)} %param.27), kind=kOutput, calls=%fused_computation.8 | convolution fusion | flops 298598400 | bytes 3110400 | tf_op jit(solution)/shard_map/dot_general | solution.py:74
  98.8 30.4 %all_to_all.11 = bf16[8,18,2880]{2,1,0:T(8,128)(2,1)S(1)} all-to-all(bf16[8,18,2880]{2,1,0:T(8,128)(2,1)S(1)} %convolution_convert_fusion), channel_id=1, replica_groups=mesh['role'=2,'grp'=8,'tp'=2] {'grp'}, dimensions={0} | all-to-all | bytes 1658880 | tf_op jit(solution)/shard_map/all_to_all | solution.py:81
  130.0 1.2 copy.70
  131.2 1.6 %dynamic-slice_convert_fusion = bf16[32,720]{1,0:T(8,128)(2,1)} fusion(f32[32,2880]{1,0:T(8,128)} %copy-done.1, s32[]{:T(128)S(6)} %select_n.37), kind=kLoop, calls=%fused_computation.32 | loop fusion | bytes 92164 | tf_op jit(solution)/shard_map/convert_element_type | solution.py:134
  132.8 19.9 %reduce-scatter.4.cloned.1.call-done = bf16[720,32]{1,0:T(8,128)(2,1)} async-done(((bf16[2880,32]{1,0:T(8,128)(2,1)}), bf16[720,32]{1,0:T(8,128)(2,1)}) %reduce-scatter.4.cloned.1.call-update) | async-done | bytes 46096
  152.7 1.7 %copy.71 = bf16[32,720]{1,0:T(8,128)(2,1)} copy(bf16[32,720]{0,1:T(8,128)(2,1)} %bitcast.69) | data formatting | bytes 92160
  (60 shorter events, 10.1 us)
Async XLA Ops:
  7.2 90.8 %copy-start = (bf16[1,360,2880]{2,1,0:T(8,128)(2,1)S(1)}, bf16[1,360,2880]{2,1,0:T(8,128)(2,1)}, u32[]{:S(2)}) copy-start(bf16[1,360,2880]{2,1,0:T(8,128)(2,1)} %param.29) | copy-start | bytes 6220804
  7.2 145.6 %reduce-scatter.4.cloned.1.call-start = ((), (), s32[]{:S(2)}) async-start(), calls=%async_computation.3 | async-start | bytes 921600
  14.0 0.7 copy-start.2
  24.6 2.6 %copy-start.5 = (pred[32,128]{1,0:T(8,128)(4,1)}, pred[32,128]{1,0:T(8,128)(4,1)S(1)}, u32[]{:S(2)}) copy-start(pred[32,128]{1,0:T(8,128)(4,1)S(1)} %fusion.28) | copy-start | bytes 12292
  28.1 2.0 %copy-start.3 = (f32[32,2,8]{2,1,0:T(2,128)}, f32[32,2,8]{2,1,0:T(2,128)S(1)}, u32[]{:S(2)}) copy-start(f32[32,2,8]{2,1,0:T(2,128)S(1)} %copy.58) | copy-start | bytes 6148
  29.4 3.0 %copy-start.6 = (pred[32,128]{1,0:T(8,128)(4,1)S(1)}, pred[32,128]{1,0:T(8,128)(4,1)}, u32[]{:S(2)}) copy-start(pred[32,128]{1,0:T(8,128)(4,1)} %copy-done.5) | copy-start | bytes 12292
  40.4 9.2 %copy-start.10 = (f32[2880]{0:T(1024)S(1)}, f32[2880]{0:T(1024)}, u32[]{:S(2)}) copy-start(f32[2880]{0:T(1024)} %param.24) | copy-start | bytes 34564
  40.4 9.3 %copy-start.9 = (bf16[720,8]{0,1:T(8,128)(2,1)S(1)}, bf16[720,8]{0,1:T(8,128)(2,1)}, u32[]{:S(2)}) copy-start(bf16[720,8]{0,1:T(8,128)(2,1)} %param.25) | copy-start | bytes 34564
  40.4 16.6 %copy-start.7 = (s32[32,4]{0,1:T(4,128)S(1)}, s32[32,4]{0,1:T(4,128)}, u32[]{:S(2)}) copy-start(s32[32,4]{0,1:T(4,128)} %param.26) | copy-start | bytes 1540
  40.5 16.7 %copy-start.4 = (pred[32,4,18]{0,2,1:T(8,128)(4,1)S(1)}, pred[32,4,18]{0,2,1:T(8,128)(4,1)}, u32[]{:S(2)}) copy-start(pred[32,4,18]{0,2,1:T(8,128)(4,1)} %iota_compare_fusion) | copy-start | bytes 6916
  40.5 16.7 %copy-start.8 = (pred[32,4,8]{0,2,1:T(8,128)(4,1)S(1)}, pred[32,4,8]{0,2,1:T(8,128)(4,1)}, u32[]{:S(2)}) copy-start(pred[32,4,8]{0,2,1:T(8,128)(4,1)} %iota_compare_fusion.1) | copy-start | bytes 3076
  49.5 8.0 %copy-start.1 = (f32[32,2880]{1,0:T(8,128)}, f32[32,2880]{1,0:T(8,128)S(1)}, u32[]{:S(2)}) copy-start(f32[32,2880]{1,0:T(8,128)S(1)} %get-tuple-element.5) | copy-start | bytes 1105924
  94.5 2.6 %copy-start.11 = (bf16[1,2880,360]{1,2,0:T(8,128)(2,1)S(1)}, bf16[1,2880,360]{1,2,0:T(8,128)(2,1)}, u32[]{:S(2)}) copy-start(bf16[1,2880,360]{1,2,0:T(8,128)(2,1)} %param.28) | copy-start | bytes 6220804
Sparse Core Ops, SparseCore 0:
  131.3 21.3 reduce-scatter.3
